TPU v7x, 32 devices: a whole 2x2x4 slice. The times are simulated.
32 devices in a mesh: pts: 8 (over z, y), hrs: 4 (over x, core).
Axes of the slice: x: 2, y: 2, z: 4, core: 2. Of those that a mesh axis runs over, the one named last changes fastest.
Arguments:
- fields: float32 [512, 65536], P(('pts', 'hrs')), may hold values from -2000 to 2000, as said below
- probes: float32 [256, 512], replicated, may hold values from -0.25 to 0.25
Outputs:
- basis_rows: float32 [256, 65536], P(None, ('pts', 'hrs'))
- coeffs: float32 [256, 512], replicated
Inputs may be any that keep to these rules, and one draw needn't show every extreme that they name: `fields`: every hour and every grid point carries its own scale, and the values are real-valued and never all zero.
All inputs are finite; a program needn't handle non-finite values.
Results may differ from a plain program's by a relative error of at most 0.00017.
Values sent between devices are 32-bit elements; how exact they have to be, the bound alone decides.
A program may use at most 64 MiB of HBM per device.

v0:
```python
import jax
import jax.numpy as jnp
from jax import lax
from jax.sharding import PartitionSpec as P

highest = lax.Precision.HIGHEST


def contract_last(left, right):
    return lax.dot_general(
        left, right, (((1,), (1,)), ((), ())), precision=highest, preferred_element_type=jnp.float32
    )


def on_device(fields, probes):
    n_pts = lax.axis_size("pts")
    n_hrs = lax.axis_size("hrs")
    panels = lax.all_to_all(fields, ("pts", "hrs"), split_axis=1, concat_axis=0, tiled=True)
    n_points = panels.shape[1] * n_pts * n_hrs
    sketched = jnp.dot(probes, panels, precision=highest, preferred_element_type=jnp.float32)
    cross_sum = lax.psum(contract_last(sketched, panels) / n_points, ("pts", "hrs"))
    local_gram = contract_last(sketched, sketched) / n_points
    gram_sum = lax.psum(local_gram, ("pts", "hrs"))
    factor = jnp.linalg.cholesky(gram_sum)
    basis_rows = lax.linalg.triangular_solve(factor, sketched, left_side=True, lower=True)
    coeffs = lax.linalg.triangular_solve(factor, cross_sum, left_side=True, lower=True)
    return (basis_rows, coeffs)


def solution(mesh):
    return jax.shard_map(
        on_device,
        mesh=mesh,
        in_specs=(P(("pts", "hrs"), None), P()),
        out_specs=(P(None, ("pts", "hrs")), P()),
        check_vma=False,
    )
```

profile of v0, /device:TPU:0, one launch (start us, length us, event | category | flops | bytes accessed | tf_op | source)
XLA Modules:
  0.0 328.4 jit_solution(12238962326394786213)
XLA Ops:
  7.2 2.5 copy.17
  9.7 100.7 %all_to_all.19 = f32[16,32,2048]{2,0,1:T(8,128)S(1)} all-to-all(f32[16,32,2048]{2,0,1:T(8,128)S(1)} %bitcast.50), channel_id=1, replica_groups=mesh['pts'=8,'hrs'=4] {'pts','hrs'}, dimensions={1} | all-to-all | bytes 8388608 | tf_op jit(solution)/shard_map/all_to_all | solution.py:18
  110.5 3.7 %fusion.13 = f32[256,2048]{1,0:T(8,128)S(1)} fusion(f32[256,512]{1,0:T(8,128)S(1)} %copy-done, f32[512,2048]{1,0:T(8,128)S(1)} %bitcast.48), kind=kOutput, calls=%fused_computation.38 | convolution fusion | flops 3221225472 | bytes 6815744 | tf_op jit(solution)/shard_map/dot_general | solution.py:20
  114.2 4.5 %convolution_multiply_fusion = f32[256,512]{1,0:T(8,128)} fusion(f32[256,2048]{1,0:T(8,128)S(1)} %fusion.13, f32[512,2048]{1,0:T(8,128)S(1)} %bitcast.49), kind=kOutput, calls=%fused_computation.5 | convolution fusion | flops 3221356544 | bytes 6815744 | tf_op jit(solution)/shard_map/dot_general | solution.py:10
  118.7 2.6 convolution_multiply_fusion.1
  121.3 129.5 %all-reduce.4.cloned.1.call-done = (f32[256,256]{0,1:T(8,128)}, f32[256,512]{1,0:T(8,128)}) async-done(((f32[256,256]{0,1:T(8,128)}, f32[256,512]{1,0:T(8,128)}), (f32[256,256]{0,1:T(8,128)}, f32[256,512]{1,0:T(8,128)})) %all-reduce.4.cloned.1.call-update) | async-done | bytes 786448 | tf_op jit(solution)/shard_map/psum | solution.py:23
  250.9 1.1 copy.13
  252.0 1.0 fusion.4
  253.0 11.9 %cholesky.50 = f32[128,128]{1,0:T(8,128)S(1)} custom-call(f32[128,128]{1,0:T(8,128)S(1)} %cholesky.118), custom_call_target="Cholesky" | custom-call | tf_op jit(solution)/shard_map/jit(cholesky)/cholesky | solution.py:24
  264.9 9.8 %custom-call.16 = f32[1,128,128]{1,2,0:T(8,128)S(1)} custom-call(f32[1,128,128]{2,1,0:T(8,128)S(1)} %get-tuple-element.25), custom_call_target="InvertDiagBlocksLowerTriangular" | custom-call | tf_op jit(solution)/shard_map/jit(cholesky)/cholesky | solution.py:24
  275.2 11.7 %cholesky.105 = f32[128,128]{1,0:T(8,128)S(1)} custom-call(f32[128,128]{1,0:T(8,128)S(1)} %convolution_subtract_fusion.2), custom_call_target="Cholesky" | custom-call | tf_op jit(solution)/shard_map/jit(cholesky)/cholesky | solution.py:24
  287.0 0.6 compare_reduce_fusion
  289.0 4.0 %while.1 = (s32[]{:T(128)}, f32[256,256]{1,0:T(8,128)S(1)}, s32[2,2]{1,0:T(2,128)S(1)}, f32[2,128,128]{2,1,0:T(8,128)S(1)}, s32[]{:T(128)}) while((s32[]{:T(128)}, f32[256,256]{1,0:T(8,128)S(1)}, s32[2,2]{1,0:T(2,128)S(1)}, f32[2,128,128]{2,1,0:T(8,128)S(1)}, s32[]{:T(128)}) %tuple.27), condition=%wide.while_cond, body=%wide.while_body.sunk | while | flops 2 | bytes 131181 | solution.py:25
  289.0 0.6 fusion.27
  289.6 1.4 bitcast_dynamic-update-slice_fusion.2
  291.6 1.4 bitcast_dynamic-update-slice_fusion.2
  293.0 19.9 %custom-call.17 = f32[2,128,128]{1,2,0:T(8,128)S(1)} custom-call(f32[2,128,128]{2,1,0:T(8,128)S(1)} %get-tuple-element.9), custom_call_target="InvertDiagBlocksLowerTriangular" | custom-call | tf_op jit(solution)/shard_map/triangular_solve | solution.py:25
  312.9 1.1 fusion
  314.0 1.4 fusion.2
  315.3 1.3 convolution_subtract_fusion.1
  317.1 0.8 pad_maximum_fusion.1
  317.9 1.0 convolution_subtract_fusion
  319.0 1.0 fusion.9
  320.0 1.5 pad_maximum_fusion
  (18 shorter events, 1.8 us)
Async XLA Ops:
  7.2 103.3 %copy-start = (f32[256,512]{1,0:T(8,128)S(1)}, f32[256,512]{1,0:T(8,128)}, u32[]{:S(2)}) copy-start(f32[256,512]{1,0:T(8,128)} %param.3) | copy-start | bytes 1572868
  7.2 243.7 %all-reduce.4.cloned.1.call-start = ((), (), s32[]{:S(2)}) async-start(), calls=%async_computation.1 | async-start | bytes 1572864 | tf_op jit(solution)/shard_map/psum | solution.py:23
Sparse Core Ops, SparseCore 0:
  121.4 129.3 all-reduce.3
where the time goes:
time: 329 us; the launch traced here: 328 us
  waiting for transfers between devices  130 us (40%)
  blocking collectives  101 us (31%)
  other arithmetic  57.4 us (17%)
  matrix products  17.5 us (5%)
  between operations  15.5 us (5%)
  local copies, waits for them, and re-layouts  7.64 us (2%)
    psum x1, waiting for transfers between devices, on_device(): gram_sum = lax.psum(local_gram, ('pts', 'hrs'))  130 us
    all_to_all x1, blocking collectives, on_device(): lax.all_to_all(fields, ('pts', 'hrs'), split_axis=1, concat_axis=0, tiled...  101 us
    another operation x6, other arithmetic, on_device(): factor = jnp.linalg.cholesky(gram_sum)  34.1 us
    another operation x4, other arithmetic, on_device(): lax.linalg.triangular_solve(factor, sketched, left_side=True, lower=True)  21.5 us
    dot_general x2, matrix products, contract_last(): lax.dot_general(left, right, (((1,), (1,)), ((), ())), precision=highest,...  7.09 us
  transfers between devices with their start and end apart: 1, of which 1 were waited for; matrix products, arithmetic and copies ran while one was open for 0% of the time, Pallas kernels for 0%

commit v1 on v0

--- a/solution.py
+++ b/solution.py
@@ -15,7 +15,15 @@
 def on_device(fields, probes):
     n_pts = lax.axis_size("pts")
     n_hrs = lax.axis_size("hrs")
-    panels = lax.all_to_all(fields, ("pts", "hrs"), split_axis=1, concat_axis=0, tiled=True)
+    panels = jnp.concatenate(
+        lax.all_to_all(
+            jnp.stack(jnp.split(fields, lax.axis_size(("pts", "hrs")), axis=1)),
+            ("pts", "hrs"),
+            0,
+            0,
+        ),
+        axis=0,
+    )
     n_points = panels.shape[1] * n_pts * n_hrs
     sketched = jnp.dot(probes, panels, precision=highest, preferred_element_type=jnp.float32)
     cross_sum = lax.psum(contract_last(sketched, panels) / n_points, ("pts", "hrs"))

time: 329 us -> 365 us (1.11)
  local copies, waits for them, and re-layouts: 7.64 us -> 34.5 us
  matrix products: 17.5 us -> 26.7 us
    unnamed x2 -> x33, local copies, waits for them, and re-layouts: 0.01 us -> 28.5 us
    dot_general x2, matrix products: 7.09 us -> 12.1 us  [contract_last(): lax.dot_general(left, right, (((1,), (1,)), ((), ())), precision=highest,...]
where the time goes in v1:
time: 365 us; the launch traced here: 364 us
  waiting for transfers between devices  130 us (36%)
  blocking collectives  101 us (28%)
  other arithmetic  57.2 us (16%)
  local copies, waits for them, and re-layouts  34.5 us (9%)
  matrix products  26.7 us (7%)
  between operations  15.6 us (4%)
    psum x1, waiting for transfers between devices, on_device(): gram_sum = lax.psum(local_gram, ('pts', 'hrs'))  130 us
    all_to_all x1, blocking collectives, on_device(): lax.all_to_all(jnp.stack(jnp.split(fields, lax.axis_size(('pts', 'hrs')),...  101 us
    another operation x6, other arithmetic, on_device(): factor = jnp.linalg.cholesky(gram_sum)  34.2 us
    unnamed x33, local copies, waits for them, and re-layouts  28.5 us
    another operation x4, other arithmetic, on_device(): lax.linalg.triangular_solve(factor, sketched, left_side=True, lower=True)  21.2 us
    dot_general x2, matrix products, contract_last(): lax.dot_general(left, right, (((1,), (1,)), ((), ())), precision=highest,...  12.1 us
  transfers between devices with their start and end apart: 1, of which 1 were waited for; matrix products, arithmetic and copies ran while one was open for 0% of the time, Pallas kernels for 0%

profile of v1, /device:TPU:0, one launch (start us, length us, event | category | flops | bytes accessed | tf_op | source)
XLA Modules:
  0.0 364.5 jit_solution(13375404520502753917)
XLA Ops:
  7.2 1.0 bitcast_dynamic-update-slice_fusion.32
  8.2 0.9 bitcast_dynamic-update-slice_fusion.31
  11.0 0.9 bitcast_dynamic-update-slice_fusion.28
  13.7 0.9 bitcast_dynamic-update-slice_fusion.25
  36.7 100.7 %all_to_all.5 = f32[32,16,2048]{2,1,0:T(8,128)S(1)} all-to-all(f32[32,16,2048]{2,1,0:T(8,128)S(1)} %bitcast_dynamic-update-slice_fusion.1), channel_id=1, replica_groups=mesh['pts'=8,'hrs'=4] {'pts','hrs'}, dimensions={0} | all-to-all | bytes 8388608 | tf_op jit(solution)/shard_map/all_to_all | solution.py:19
  137.5 7.1 %fusion.13 = f32[2048,256]{1,0:T(8,128)S(1)} fusion(f32[512,2048]{1,0:T(8,128)S(1)} %bitcast.109, f32[256,512]{1,0:T(8,128)S(1)} %copy-done), kind=kOutput, calls=%fused_computation.69 | convolution fusion | flops 3221225472 | bytes 6815744 | tf_op jit(solution)/shard_map/dot_general | solution.py:28
  144.6 7.9 %convolution_multiply_fusion = f32[256,512]{1,0:T(8,128)} fusion(f32[2048,256]{1,0:T(8,128)S(1)} %fusion.13, f32[512,2048]{1,0:T(8,128)S(1)} %bitcast.110), kind=kOutput, calls=%fused_computation.4 | convolution fusion | flops 3221356544 | bytes 6815744 | tf_op jit(solution)/shard_map/dot_general | solution.py:10
  152.5 4.2 %convolution_multiply_fusion.1 = f32[256,256]{0,1:T(8,128)} fusion(f32[2048,256]{1,0:T(8,128)S(1)} %fusion.13), kind=kOutput, calls=%fused_computation.6 | convolution fusion | flops 1610678272 | bytes 2359296 | tf_op jit(solution)/shard_map/dot_general | solution.py:10
  156.7 129.5 %all-reduce.4.cloned.1.call-done = (f32[256,256]{0,1:T(8,128)}, f32[256,512]{1,0:T(8,128)}) async-done(((f32[256,256]{0,1:T(8,128)}, f32[256,512]{1,0:T(8,128)}), (f32[256,256]{0,1:T(8,128)}, f32[256,512]{1,0:T(8,128)})) %all-reduce.4.cloned.1.call-update) | async-done | bytes 786448 | tf_op jit(solution)/shard_map/psum | solution.py:31
  286.3 1.1 copy.5
  287.4 1.0 fusion.4
  288.4 11.7 %cholesky.50 = f32[128,128]{1,0:T(8,128)S(1)} custom-call(f32[128,128]{1,0:T(8,128)S(1)} %cholesky.118), custom_call_target="Cholesky" | custom-call | tf_op jit(solution)/shard_map/jit(cholesky)/cholesky | solution.py:32
  300.1 9.8 %custom-call.16 = f32[1,128,128]{1,2,0:T(8,128)S(1)} custom-call(f32[1,128,128]{2,1,0:T(8,128)S(1)} %get-tuple-element.25), custom_call_target="InvertDiagBlocksLowerTriangular" | custom-call | tf_op jit(solution)/shard_map/jit(cholesky)/cholesky | solution.py:32
  310.4 11.9 %cholesky.105 = f32[128,128]{1,0:T(8,128)S(1)} custom-call(f32[128,128]{1,0:T(8,128)S(1)} %convolution_subtract_fusion.2), custom_call_target="Cholesky" | custom-call | tf_op jit(solution)/shard_map/jit(cholesky)/cholesky | solution.py:32
  324.4 4.0 %while.1 = (s32[]{:T(128)}, f32[256,256]{1,0:T(8,128)S(1)}, s32[2,2]{1,0:T(2,128)S(1)}, f32[2,128,128]{2,1,0:T(8,128)S(1)}, s32[]{:T(128)}) while((s32[]{:T(128)}, f32[256,256]{1,0:T(8,128)S(1)}, s32[2,2]{1,0:T(2,128)S(1)}, f32[2,128,128]{2,1,0:T(8,128)S(1)}, s32[]{:T(128)}) %tuple.27), condition=%wide.while_cond, body=%wide.while_body.sunk | while | flops 2 | bytes 131181 | solution.py:33
  325.0 1.4 bitcast_dynamic-update-slice_fusion.34
  327.0 1.4 bitcast_dynamic-update-slice_fusion.34
  328.4 19.7 %custom-call.17 = f32[2,128,128]{1,2,0:T(8,128)S(1)} custom-call(f32[2,128,128]{2,1,0:T(8,128)S(1)} %get-tuple-element.9), custom_call_target="InvertDiagBlocksLowerTriangular" | custom-call | tf_op jit(solution)/shard_map/triangular_solve | solution.py:33
  348.1 1.4 fusion.2
  349.5 1.3 convolution_subtract_fusion.1
  352.1 1.1 fusion
  353.2 1.8 convolution_subtract_fusion
  355.0 1.1 fusion.9
  356.1 1.5 pad_maximum_fusion
  (49 shorter events, 29.5 us)
Async XLA Ops:
  7.2 130.3 %copy-start = (f32[256,512]{1,0:T(8,128)S(1)}, f32[256,512]{1,0:T(8,128)}, u32[]{:S(2)}) copy-start(f32[256,512]{1,0:T(8,128)} %param.3) | copy-start | bytes 1572868
  7.2 279.1 %all-reduce.4.cloned.1.call-start = ((), (), s32[]{:S(2)}) async-start(), calls=%async_computation.1 | async-start | bytes 1572864 | tf_op jit(solution)/shard_map/psum | solution.py:31
Sparse Core Ops, SparseCore 0:
  156.8 129.3 all-reduce.3
